TPU v7x, 128 devices: a whole 4x4x4 slice. The times are simulated.
128 devices in a mesh: dp: 1, ep: 128 (over z, y, x, core).
Axes of the slice: x: 4, y: 4, z: 4, core: 2. Of those that a mesh axis runs over, the one named last changes fastest.
Arguments:
- hidden: bfloat16 [65536, 768], P(('dp', 'ep'))
- logits: float32 [65536, 128], P(('dp', 'ep'))
- w_in: bfloat16 [128, 768, 3072], P('ep')
- w_out: bfloat16 [128, 3072, 768], P('ep')
Outputs:
- output: bfloat16 [65536, 768], P(('dp', 'ep'))
All inputs are finite; a program needn't handle non-finite values.
Results may differ from a plain program's by a relative error of at most 0.00468909.
Values are sent between devices in bfloat16 or wider.
A program may use at most 1 GiB of HBM per device.

v0:
```python
import jax
import jax.numpy as jnp
from jax import lax
from jax.sharding import PartitionSpec as P

CAP_FACTOR = 2


def solution(mesh):
    n_group = mesh.shape["ep"]

    def local_layer(hidden, logits, w_in, w_out):
        tok_dev, d_model = hidden.shape
        n_experts = logits.shape[1]
        local_exp = w_in.shape[0]
        half_tok = tok_dev // 2
        per_src = tok_dev * CAP_FACTOR // n_experts
        capacity = n_group * per_src // 2
        pool_len = n_group * per_src

        def by_owner(array_in):
            return array_in.reshape(2, n_group, local_exp, per_src).transpose(2, 0, 1, 3)

        gate_probs = jax.nn.softmax(logits, axis=-1)
        logit_cols = jnp.swapaxes(logits.reshape(2, half_tok, n_experts), 1, 2)
        gate_cols = jnp.swapaxes(gate_probs.reshape(2, half_tok, n_experts), 1, 2)
        cand_val, cand_pos = lax.top_k(logit_cols, per_src)
        cand_gate = by_owner(jnp.take_along_axis(gate_cols, cand_pos, axis=2))
        row_ids = by_owner(cand_pos + (jnp.arange(2) * half_tok)[:, None, None])
        send_rows = jnp.take(hidden, row_ids, axis=0)

        pool_val = lax.all_to_all(by_owner(cand_val), "ep", 2, 2, tiled=True)
        pool_rows = lax.all_to_all(send_rows, "ep", 2, 2, tiled=True)

        pick_pos = lax.top_k(pool_val.reshape(local_exp, 2, pool_len), capacity)[1]
        flat_ids = (jnp.arange(local_exp * 2).reshape(local_exp, 2, 1) * pool_len + pick_pos).reshape(-1)
        picked_rows = jnp.take(pool_rows.reshape(-1, d_model), flat_ids, axis=0).reshape(local_exp, 2, capacity, d_model)
        pre_act = jnp.einsum("emcd,edf->emcf", picked_rows, w_in, preferred_element_type=jnp.float32)
        hidden_act = jax.nn.gelu(pre_act, approximate=True).astype(jnp.bfloat16)
        expert_out = jnp.einsum("emcf,efd->emcd", hidden_act, w_out, preferred_element_type=jnp.float32).astype(jnp.bfloat16)
        ret_rows = jnp.zeros((local_exp * 2 * pool_len, d_model), jnp.bfloat16).at[flat_ids].set(expert_out.reshape(-1, d_model), unique_indices=True)
        ret_rows = ret_rows.reshape(local_exp, 2, n_group, per_src, d_model)

        back_rows = lax.all_to_all(ret_rows, "ep", 2, 2, tiled=True)
        weighted = back_rows.astype(jnp.float32) * cand_gate[..., None]
        mixed = jax.ops.segment_sum(weighted.reshape(-1, d_model), row_ids.reshape(-1), num_segments=tok_dev)
        return (hidden.astype(jnp.float32) + mixed).astype(jnp.bfloat16)

    tok_spec = P(("dp", "ep"), None)
    exp_spec = P("ep", None, None)
    return jax.shard_map(local_layer, mesh=mesh, in_specs=(tok_spec, tok_spec, exp_spec, exp_spec), out_specs=tok_spec, check_vma=False)
```

profile of v0, /device:TPU:1, one launch (start us, length us, event | category | flops | bytes accessed | tf_op | source)
XLA Modules:
  0.0 200.1 jit_solution(2327228142521214171)
XLA Ops:
  0.0 0.0 copy-start
  0.0 6.9 %top_k.18 = (f32[2,128,256]{1,2,0:T(8,128)S(1)}, s32[2,128,256]{1,2,0:T(8,128)S(1)}) sort(f32[2,128,256]{1,2,0:T(8,128)} %bitcast.46, s32[2,128,256]{1,2,0:T(8,128)S(1)} %top_k.17.clone), dimensions={2}, to_apply=%region_0.0 | sort | flops 1048576 | bytes 1048576 | tf_op jit(solution)/shard_map/top_k | solution.py:27
  7.0 0.1 copy.37
  7.1 0.8 copy.24
  7.9 11.5 %all-to-all-start = ((f32[1,2,128,8]{3,1,0,2:T(2,128)}), f32[1,2,128,8]{3,1,0,2:T(2,128)S(1)}, u32[]{:S(2)}, u32[]{:S(2)}) async-start(f32[1,2,128,8]{3,1,0,2:T(2,128)} %copy.24), calls=%async_computation | async-start | bytes 262144 | tf_op jit(solution)/shard_map/all_to_all | solution.py:32
  19.4 0.1 compare_and_fusion
  19.5 0.1 copy.27
  19.6 0.1 reshape.180
  19.7 0.2 copy.26
  19.9 0.0 copy-done
  19.9 9.4 %gather_fusion = bf16[2048,768]{1,0:T(8,128)(2,1)} fusion(bf16[512,768]{1,0:T(8,128)(2,1)S(1)} %copy-done, s32[2048]{0:T(1024)S(1)} %broadcast_clamp_fusion), kind=kCustom, calls=%fused_computation | custom fusion | bytes 6299648 | tf_op jit(solution)/shard_map/jit(_take)/gather | solution.py:30
  29.3 3.3 %copy_select_fusion = bf16[1,2,128,8,768]{4,3,1,0,2:T(8,128)(2,1)} fusion(bf16[1,2,128,8,768]{4,3,2,1,0:T(8,128)(2,1)} %bitcast.44, pred[2,128,8]{2,0,1:T(4,128)(4,1)S(1)} %copy.26), kind=kLoop, calls=%fused_computation.19 | loop fusion | flops 1572864 | bytes 6293504 | tf_op jit(solution)/shard_map/jit(_take)/select_n | solution.py:30
  32.6 0.0 all-to-all-done
  32.7 10.2 %all-to-all-start.1 = ((bf16[1,2,128,8,768]{4,3,1,0,2:T(8,128)(2,1)}), bf16[1,2,128,8,768]{4,3,1,0,2:T(8,128)(2,1)}, u32[]{:S(2)}, u32[]{:S(2)}) async-start(bf16[1,2,128,8,768]{4,3,1,0,2:T(8,128)(2,1)} %copy_select_fusion), calls=%async_computation.1 | async-start | bytes 6291456 | tf_op jit(solution)/shard_map/all_to_all | solution.py:33
  42.9 0.1 reshape.167
  43.0 4.8 %top_k.26 = (f32[1,2,1024]{2,1,0:T(2,128)}, s32[1,2,1024]{2,1,0:T(2,128)S(1)}) sort(f32[1,2,1024]{2,1,0:T(2,128)S(1)} %reshape.167, s32[1,2,1024]{2,1,0:T(2,128)S(1)} %top_k.25), dimensions={2}, to_apply=%region_1.0 | sort | flops 22528 | bytes 32768 | tf_op jit(solution)/shard_map/top_k | solution.py:35
  47.8 0.1 fusion.22
  47.8 0.1 compare_and_fusion.1
  48.0 39.7 %all-to-all-done.1 = bf16[1,2,128,8,768]{4,3,1,0,2:T(8,128)(2,1)} async-done(((bf16[1,2,128,8,768]{4,3,1,0,2:T(8,128)(2,1)}), bf16[1,2,128,8,768]{4,3,1,0,2:T(8,128)(2,1)}, u32[]{:S(2)}, u32[]{:S(2)}) %all-to-all-start.1) | async-done | bytes 3145760 | tf_op jit(solution)/shard_map/all_to_all | solution.py:33
  87.7 3.8 %copy.29 = bf16[1,2,128,8,768]{4,3,2,1,0:T(8,128)(2,1)} copy(bf16[1,2,128,8,768]{4,3,1,0,2:T(8,128)(2,1)} %all-to-all-done.1) | data formatting | bytes 6291456 | tf_op jit(solution)/shard_map/all_to_all | solution.py:33
  91.5 6.8 %gather_fusion.1 = bf16[1024,768]{1,0:T(8,128)(2,1)S(1)} fusion(bf16[2048,768]{1,0:T(8,128)(2,1)} %bitcast.42, s32[1024]{0:T(1024)S(1)} %broadcast_clamp_fusion.1), kind=kCustom, calls=%fused_computation.1 | custom fusion | bytes 3149824 | tf_op jit(solution)/shard_map/jit(_take)/gather | solution.py:37
  98.3 0.0 slice-start
  98.3 0.2 broadcast_select_fusion
  98.5 0.0 slice-start.1
  98.5 7.1 %fusion.11 = f32[2,512,3072]{2,1,0:T(8,128)S(1)} fusion(bf16[2,512,768]{2,1,0:T(8,128)(2,1)S(1)} %bitcast.47, bf16[1,768,3072]{2,1,0:T(8,128)(2,1)} %param.6), kind=kOutput, calls=%fused_computation.17 | convolution fusion | flops 4831838208 | bytes 18874368 | tf_op jit(solution)/shard_map/emcd,edf->emcf/dot_general | solution.py:38
  105.6 0.0 slice-done
  105.6 0.0 slice-done.1
  105.6 7.5 %fusion.13 = bf16[2,512,768]{2,1,0:T(8,128)(2,1)S(1)} fusion(bf16[1,3072,768]{2,1,0:T(8,128)(2,1)S(1)} %bitcast.52, f32[2,512,3072]{2,1,0:T(8,128)S(1)} %fusion.11), kind=kOutput, calls=%fused_computation.20 | convolution fusion | flops 4860936192 | bytes 18874368 | tf_op jit(solution)/shard_map/emcf,efd->emcd/dot_general | solution.py:40
  113.2 7.4 %scatter_custom_fusion = bf16[2048,768]{1,0:T(8,128)(2,1)} fusion(s32[1024]{0:T(1024)S(1)} %bitcast.49, bf16[1024,768]{1,0:T(8,128)(2,1)S(1)} %bitcast.53, bf16[]{:T(256)} %constant.41.clone.1), kind=kCustom, calls=%fused_computation.21 | custom fusion | bytes 3145730 | tf_op jit(solution)/shard_map/scatter | solution.py:41
  120.5 3.8 %copy.30 = bf16[1,2,128,8,768]{4,3,1,0,2:T(8,128)(2,1)} copy(bf16[1,2,128,8,768]{4,3,2,1,0:T(8,128)(2,1)} %bitcast.45) | data formatting | bytes 6291456 | tf_op jit(solution)/shard_map/reshape | solution.py:42
  124.3 0.0 copy-start.1
  124.3 6.5 %all-to-all-start.2 = ((bf16[1,2,128,8,768]{4,3,1,0,2:T(8,128)(2,1)}), bf16[1,2,128,8,768]{4,3,1,0,2:T(8,128)(2,1)}, u32[]{:S(2)}, u32[]{:S(2)}) async-start(bf16[1,2,128,8,768]{4,3,1,0,2:T(8,128)(2,1)} %copy.30), calls=%async_computation.2 | async-start | bytes 6291456 | tf_op jit(solution)/shard_map/all_to_all | solution.py:44
  130.9 0.1 copy.23
  131.0 0.1 convert_element_type.17
  131.1 0.1 copy.32
  131.3 0.1 reshape.194
  131.4 0.0 copy-done.1
  131.4 0.1 reduce_max.9
  131.5 0.2 fusion.21
  131.8 0.2 fusion.20
  132.0 16.9 %gather_fusion.2 = f32[2048]{0:T(1024)S(1)} fusion(f32[2,128,256]{1,2,0:T(8,128)S(1)} %bitcast.41, s32[2048]{0:T(1024)S(1)} %reshape.194), kind=kCustom, calls=%fused_computation.2 | custom fusion | bytes 40960 | tf_op jit(solution)/shard_map/jit(take_along_axis)/gather | solution.py:28
  148.8 0.1 reshape.197
  149.0 0.1 copy.33
  149.0 0.1 copy.34
  149.2 0.1 reshape.210
  149.3 29.7 %all-to-all-done.2 = bf16[1,2,128,8,768]{4,3,1,0,2:T(8,128)(2,1)} async-done(((bf16[1,2,128,8,768]{4,3,1,0,2:T(8,128)(2,1)}), bf16[1,2,128,8,768]{4,3,1,0,2:T(8,128)(2,1)}, u32[]{:S(2)}, u32[]{:S(2)}) %all-to-all-start.2) | async-done | bytes 3145760 | tf_op jit(solution)/shard_map/all_to_all | solution.py:44
  178.9 5.1 %convert_multiply_fusion = f32[1,2,128,8,768]{4,3,2,1,0:T(8,128)} fusion(bf16[1,2,128,8,768]{4,3,1,0,2:T(8,128)(2,1)} %all-to-all-done.2, f32[2,128,8]{2,1,0:T(8,128)S(1)} %copy.34), kind=kLoop, calls=%fused_computation.14 | loop fusion | flops 3145728 | bytes 9445376 | tf_op jit(solution)/shard_map/mul | solution.py:45
  184.1 15.1 %scatter_fusion = f32[512,768]{1,0:T(8,128)S(1)} fusion(f32[512,768]{1,0:T(8,128)S(1)} %convert_element_type.17, s32[2048]{0:T(1024)S(1)} %reshape.210, f32[2048,768]{1,0:T(8,128)} %bitcast.43), kind=kCustom, calls=%fused_computation.4 | custom fusion | flops 1572864 | bytes 18882560 | tf_op jit(solution)/shard_map/scatter-add | solution.py:46
  199.1 1.0 convert_element_type.21
  (15 shorter events, 0.1 us)
Async XLA Ops:
  0.0 19.9 %copy-start = (bf16[512,768]{1,0:T(8,128)(2,1)S(1)}, bf16[512,768]{1,0:T(8,128)(2,1)}, u32[]{:S(2)}) copy-start(bf16[512,768]{1,0:T(8,128)(2,1)} %param.4) | copy-start | bytes 2359300
  7.9 24.8 %all-to-all-start = ((f32[1,2,128,8]{3,1,0,2:T(2,128)}), f32[1,2,128,8]{3,1,0,2:T(2,128)S(1)}, u32[]{:S(2)}, u32[]{:S(2)}) async-start(f32[1,2,128,8]{3,1,0,2:T(2,128)} %copy.24), calls=%async_computation | async-start | bytes 262144 | tf_op jit(solution)/shard_map/all_to_all | solution.py:32
  32.7 55.1 %all-to-all-start.1 = ((bf16[1,2,128,8,768]{4,3,1,0,2:T(8,128)(2,1)}), bf16[1,2,128,8,768]{4,3,1,0,2:T(8,128)(2,1)}, u32[]{:S(2)}, u32[]{:S(2)}) async-start(bf16[1,2,128,8,768]{4,3,1,0,2:T(8,128)(2,1)} %copy_select_fusion), calls=%async_computation.1 | async-start | bytes 6291456 | tf_op jit(solution)/shard_map/all_to_all | solution.py:33
  98.3 7.3 %slice-start = ((s8[4718592]{0:T(1024)(128)(4,1)}), s8[4194304]{0:T(1024)(128)(4,1)S(1)}, s32[]{:S(2)}) async-start(s8[4718592]{0:T(1024)(128)(4,1)} %bitcast.51), calls=%async_computation.3 | async-start | bytes 8388608
  98.5 7.1 %slice-start.1 = ((s8[4718592]{0:T(1024)(128)(4,1)}), s8[524288]{0:T(1024)(128)(4,1)S(1)}, s32[]{:S(2)}) async-start(s8[4718592]{0:T(1024)(128)(4,1)} %bitcast.51), calls=%async_computation.4 | async-start | bytes 1048576
  124.3 7.0 %copy-start.1 = (f32[512,128]{1,0:T(8,128)S(1)}, f32[512,128]{1,0:T(8,128)}, u32[]{:S(2)}) copy-start(f32[512,128]{1,0:T(8,128)} %param.5) | copy-start | bytes 786436
  124.3 54.6 %all-to-all-start.2 = ((bf16[1,2,128,8,768]{4,3,1,0,2:T(8,128)(2,1)}), bf16[1,2,128,8,768]{4,3,1,0,2:T(8,128)(2,1)}, u32[]{:S(2)}, u32[]{:S(2)}) async-start(bf16[1,2,128,8,768]{4,3,1,0,2:T(8,128)(2,1)} %copy.30), calls=%async_computation.2 | async-start | bytes 6291456 | tf_op jit(solution)/shard_map/all_to_all | solution.py:44
where the time goes:
time: 201 us; the launch traced here: 200 us
  waiting for transfers between devices  69.4 us (35%)
  local copies, waits for them, and re-layouts  50.2 us (25%)
  other arithmetic  37.4 us (19%)
  starting transfers between devices  28.2 us (14%)
  matrix products  14.6 us (7%)
    all_to_all x1, waiting for transfers between devices, local_layer(): pool_rows = lax.all_to_all(send_rows, 'ep', 2, 2, tiled=True)  39.7 us
    all_to_all x1, waiting for transfers between devices, local_layer(): back_rows = lax.all_to_all(ret_rows, 'ep', 2, 2, tiled=True)  29.7 us
    gather x5, local copies, waits for them, and re-layouts, local_layer(): cand_gate = by_owner(jnp.take_along_axis(gate_cols, cand_pos, axis=2))  17.2 us
    scatter-add x1, other arithmetic, local_layer(): jax.ops.segment_sum(weighted.reshape(-1, d_model), row_ids.reshape(-1), n...  15.1 us
    all_to_all x1, starting transfers between devices, local_layer(): pool_val = lax.all_to_all(by_owner(cand_val), 'ep', 2, 2, tiled=True)  11.5 us
    all_to_all x1, starting transfers between devices, local_layer(): pool_rows = lax.all_to_all(send_rows, 'ep', 2, 2, tiled=True)  10.2 us
    gather x1, local copies, waits for them, and re-layouts, local_layer(): send_rows = jnp.take(hidden, row_ids, axis=0)  9.38 us
    dot_general x1, matrix products, local_layer(): jnp.einsum('emcf,efd->emcd', hidden_act, w_out, preferred_element_type=jn...  7.55 us
  transfers between devices with their start and end apart: 3, of which 2 were waited for; matrix products, arithmetic and copies ran while one was open for 18% of the time, Pallas kernels for 0%

commit v1 on v0

v1 whole, which is shorter than its diff:
```python
import functools
import math

import jax
import jax.numpy as jnp
from jax import lax
from jax.experimental import pallas as pl
from jax.experimental.pallas import tpu as pltpu
from jax.sharding import PartitionSpec as P

MESH = pl.DeviceIdType.MESH
BF16, F32 = jnp.bfloat16, jnp.float32
NDEV = 128
RANKS = 8
KEEP = 512
ORDERS = ((2, 1, 0), (1, 0, 2), (0, 2, 1))
NPART = 3
NCHUNK = 4
FSTEPS = 6


def coords(d):
    return lax.div(d, 32), lax.rem(lax.div(d, 8), 4), lax.rem(lax.div(d, 2), 4), lax.rem(d, 2)


def shifted(me, offs, core):
    pos = coords(me)
    z, y, x = (lax.rem(p + (o + 4), 4) for p, o in zip(pos[:3], offs))
    return (z * 4 + y) * 8 + x * 2 + lax.rem(pos[3] + core, 2)


def along(dim, step):
    return tuple(step if d == dim else 0 for d in range(3))


def gelu(v):
    inner = v * (0.7978845608028654 + 0.035677408136300125 * (v * v))
    half = 0.5 * v
    return half + half * jnp.tanh(inner)


def split3(v):
    a = v.astype(BF16)
    r = v - a.astype(F32)
    b = r.astype(BF16)
    c = (r - b.astype(F32)).astype(BF16)
    return a, b, c


def dot(a, b):
    return jnp.dot(a, b, preferred_element_type=F32)


def dot_t(a, b):
    return lax.dot_general(a, b, (((1,), (1,)), ((), ())), preferred_element_type=F32)


class Exchange:
    def __init__(self, me, sign, hop, mids, final, send_sem, recv_sem, cols):
        self.me, self.sign, self.hop, self.mids, self.final = me, sign, hop, mids, final
        self.send_sem, self.recv_sem, self.cols = send_sem, recv_sem, cols
        self.peers = {}
        for core in range(2):
            for dim in range(3):
                for d in range(4):
                    self.peers[dim, d, core] = shifted(me, along(dim, sign * d), core)

    def sem(self, c, p, phase):
        return (c * NPART + p) * 3 + phase

    def copy(self, src, dst, c, p, phase, d, core):
        to = self.peers[ORDERS[p][phase], d, core]
        k = self.sem(c, p, phase)
        pltpu.make_async_remote_copy(
            src, dst, self.send_sem.at[k], self.recv_sem.at[k], device_id=(0, to), device_id_type=MESH
        ).start()

    def mid_at(self, p, c, d1):
        mid = self.mids[p]
        if ORDERS[p][1] < ORDERS[p][0]:
            return mid.at[c, d1 - 1]
        return mid.at[c, :, d1 - 1]

    def final_at(self, c, p, pick):
        idx = tuple(pick[ORDERS[p].index(d)] for d in range(3))
        return self.final.at[(c, *idx, slice(None), pl.ds(p * self.cols, self.cols))]

    def send0(self, c, p):
        for d in (1, 3, 2):
            self.copy(self.hop.at[c, p, d - 1], self.hop.at[c, p, 3 + d], c, p, 0, d, 0)

    def send1(self, c, p):
        for d in (1, 3, 2):
            self.copy(self.hop.at[c, p, pl.ds(3, 4), d], self.mid_at(p, c, d), c, p, 1, d, 0)

    def send2(self, c, p):
        core = c % 2
        for d in (1, 3, 2, 0):
            if d == 0 and core == 0:
                continue
            self.copy(self.hop.at[c, p, pl.ds(3, 4), 0, d], self.final_at(c, p, (pl.ds(0, 4), 0, d)), c, p, 2, d, core)
            self.copy(self.mids[p].at[c, :, :, d], self.final_at(c, p, (pl.ds(0, 4), pl.ds(1, 3), d)), c, p, 2, d, core)

    def own(self, c, p):
        self.final_set(c, p, (pl.ds(0, 4), 0, 0), self.hop[c, p, pl.ds(3, 4), 0, 0])
        self.final_set(c, p, (pl.ds(0, 4), pl.ds(1, 3), 0), self.mids[p][c, :, :, 0])

    def final_set(self, c, p, pick, value):
        idx = tuple(pick[ORDERS[p].index(d)] for d in range(3))
        self.final[(c, *idx, slice(None), pl.ds(p * self.cols, self.cols))] = value

    def region(self, c, p, phase):
        if phase == 0:
            return self.hop.at[c, p, pl.ds(4, 3)]
        if phase == 1:
            return self.mids[p].at[c]
        part = pl.ds(0, 4) if c % 2 else pl.ds(1, 3)
        return self.final_at(c, p, (pl.ds(0, 4), pl.ds(0, 4), part))

    def wait_recv(self, c, p, phase):
        r = self.region(c, p, phase)
        pltpu.make_async_copy(r, r, self.recv_sem.at[self.sem(c, p, phase)]).wait()

    def wait_send(self, c, p, phase):
        r = self.region(c, p, phase)
        pltpu.make_async_copy(r, r, self.send_sem.at[self.sem(c, p, phase)]).wait()

    def first(self, c):
        for p in range(NPART):
            self.send0(c, p)

    def second(self, c):
        for p in range(NPART):
            self.wait_recv(c, p, 0)
            self.send1(c, p)

    def third(self, c):
        for p in range(NPART):
            self.wait_recv(c, p, 1)
            self.send2(c, p)

    def arrived(self, c):
        for p in range(NPART):
            self.wait_recv(c, p, 2)
            if c % 2 == 0:
                self.own(c, p)

    def drain(self):
        for c in range(NCHUNK):
            for p in range(NPART):
                for phase in range(3):
                    self.wait_send(c, p, phase)


def kernel(
    x_hbm, l_hbm, win_hbm, wout_hbm, out_ref,
    x_ref, l_ref, win, wout, hop_i, mid_i0, mid_i1, mid_i2, fin_i, hop_r, mid_r0, mid_r1, mid_r2, fin_r,
    place, comb, mask, tops, vsend, vrecv, rank, acc, yacc,
    load_sem, send_i, recv_i, send_r, recv_r, vsend_sem, vrecv_sem,
):
    me = lax.axis_index("ep")
    half, n_exp = l_ref.shape[0] // 2, l_ref.shape[1]
    d_model, ff = win.shape
    cols = d_model // NPART
    ftile = ff // FSTEPS
    rows = 64 * RANKS

    loads = [
        pltpu.make_async_copy(s, d, load_sem.at[i])
        for i, (s, d) in enumerate(((l_hbm, l_ref), (x_hbm, x_ref), (win_hbm.at[0], win), (wout_hbm.at[0], wout)))
    ]
    for ld in loads:
        ld.start()

    barrier = pltpu.get_barrier_semaphore()

    def hello(k, _):
        pl.semaphore_signal(barrier, inc=1, device_id=(0, lax.rem(me + k, NDEV)), device_id_type=MESH)
        return 0

    lax.fori_loop(1, NDEV, hello, 0)

    inward = Exchange(me, 1, hop_i, (mid_i0, mid_i1, mid_i2), fin_i, send_i, recv_i, cols)
    back = Exchange(me, -1, hop_r, (mid_r0, mid_r1, mid_r2), fin_r, send_r, recv_r, cols)

    pos = coords(me)
    for core in range(2):
        q = lax.broadcasted_iota(jnp.int32, (rows, n_exp), 0)
        e = lax.broadcasted_iota(jnp.int32, (rows, n_exp), 1)
        ez = ((q >> 7) + pos[0]) & 3
        ey = ((q >> 5) + pos[1]) & 3
        ex = ((q >> 3) + pos[2]) & 3
        ec = (pos[3] + core) & 1
        want = ez * 32 + ey * 8 + ex * 2 + ec
        place[core] = jnp.where(e == want, 1.0, 0.0).astype(BF16)

    def put_blocks(dst, c, value):
        for z in range(4):
            for y in range(4):
                at = (z * 4 + y) * 32
                xs = value[at : at + 32, :].reshape(4, 8, d_model).astype(BF16)
                p0, p1, p2 = (xs[:, :, p * cols : (p + 1) * cols] for p in range(NPART))
                dst[c, 0, pl.ds(0, 3), y, z] = p0[1:]
                dst[c, 0, 3, y, z] = p0[0]
                dst[c, 1, (y + 3) % 4, z] = p1
                dst[c, 2, (z + 3) % 4, :, y] = p2

    loads[0].wait()
    tops[...] = jnp.zeros_like(tops)
    for m in range(2):
        cur = l_ref[m * half : (m + 1) * half, :]
        rk = jnp.full(cur.shape, 15.0, F32)
        for r in range(RANKS):
            top = jnp.max(cur, axis=0, keepdims=True)
            hit = cur == top
            rk = jnp.where(hit, float(r), rk)
            cur = jnp.where(hit, -1e30, cur)
            tops[m * RANKS + r : m * RANKS + r + 1, :] = top
        rank[m] = rk.astype(BF16)
        if m == 0:
            loads[1].wait()
        for core in range(2):
            wide = dot_t(place[core], rank[m])
            r_of = (lax.broadcasted_iota(jnp.int32, wide.shape, 0) & 7).astype(F32)
            pick = jnp.where(wide == r_of, 1.0, 0.0).astype(BF16)
            put_blocks(hop_i, m * 2 + core, dot(pick, x_ref[m * half : (m + 1) * half, :]))
        if m == 0:
            pl.semaphore_wait(barrier, NDEV - 1)
            inward.first(0)
            inward.first(1)

    eye = jnp.where(
        lax.broadcasted_iota(jnp.int32, (n_exp, n_exp), 0) == lax.broadcasted_iota(jnp.int32, (n_exp, n_exp), 1), 1.0, 0.0
    ).astype(BF16)
    hi, mid, low = (dot_t(eye, v) for v in split3(tops[...]))
    vsend[...] = ((hi + mid) + low).reshape(n_exp, 1, n_exp)

    inward.second(0)
    inward.first(2)

    def tell(k, _):
        kz, ky, kx, kc = coords(k)
        to = shifted(me, (kz, ky, kx), kc)
        pltpu.make_async_remote_copy(
            vsend.at[to], vrecv.at[k], vsend_sem, vrecv_sem, device_id=(0, to), device_id_type=MESH
        ).start()
        return 0

    lax.fori_loop(1, NDEV, tell, 0)
    vrecv[0] = vsend[me]

    inward.second(1)

    for m in range(2):
        lg = l_ref[m * half : (m + 1) * half, :]
        ex = jnp.exp(lg - jnp.max(lg, axis=1, keepdims=True))
        terms = split3(ex / jnp.sum(ex, axis=1, keepdims=True))
        for core in range(2):
            wide = dot_t(rank[m], place[core])
            r_of = (lax.broadcasted_iota(jnp.int32, wide.shape, 1) & 7).astype(F32)
            hit = wide == r_of
            for i, term in enumerate(terms):
                comb[m * 2 + core, i] = jnp.where(hit, dot_t(term, place[core]), 0.0).astype(BF16)
        if m == 0:
            inward.third(0)
            inward.first(3)

    inward.second(2)

    told = vrecv.at[pl.ds(1, NDEV - 1)]
    pltpu.make_async_copy(told, told, vrecv_sem).wait()
    seen = vrecv[...].reshape(NDEV, n_exp)
    lane = lax.broadcasted_iota(jnp.int32, (NDEV, n_exp), 1)
    cut = None
    for m in range(2):
        mine = (lane >> 3) == m

        def bisect(_, state):
            low_end, width = state
            cand = low_end + width
            cnt = jnp.sum(jnp.where(mine & (seen >= cand), 1.0, 0.0), axis=0, keepdims=True)
            cnt = jnp.sum(cnt, axis=1, keepdims=True)
            return jnp.where(cnt >= float(KEEP), cand, low_end), width * 0.5

        t = lax.fori_loop(0, 24, bisect, (jnp.full((1, 1), -8.0, F32), jnp.full((1, 1), 8.0, F32)))[0]
        cut = t if m == 0 else jnp.where((lane >> 3) == 0, cut, t)
    chosen = jnp.where(seen >= cut, 1.0, 0.0).astype(BF16)
    for core in range(2):
        q = lax.broadcasted_iota(jnp.int32, (rows, NDEV), 0)
        src = lax.broadcasted_iota(jnp.int32, (rows, NDEV), 1)
        wide = dot(jnp.where(src == (q >> 3) * 2 + core, 1.0, 0.0).astype(BF16), chosen)
        for m in range(2):
            keep = jnp.where(src == (q & 7) + m * 8, wide, 0.0)
            mask[m * 2 + core] = jnp.sum(keep, axis=1, keepdims=True)

    inward.third(1)
    loads[2].wait()
    loads[3].wait()

    def combine(c):
        back.arrived(c)
        m, core = c // 2, c % 2
        y = fin_r[c].reshape(rows, d_model)
        total = dot(comb[c, 0], y) + dot(comb[c, 1], y) + dot(comb[c, 2], y)
        if core == 0:
            yacc[m] = total
        else:
            both = x_ref[m * half : (m + 1) * half, :].astype(F32) + (yacc[m] + total)
            out_ref[m * half : (m + 1) * half, :] = both.astype(BF16)

    during = {
        1: [lambda: inward.second(3)],
        3: [lambda: inward.third(2)],
        7: [lambda: inward.third(3)],
        12: [lambda: back.second(0)],
        15: [lambda: back.second(1)],
        17: [lambda: back.third(0)],
        19: [lambda: back.third(1)],
        21: [lambda: combine(0)],
        22: [lambda: back.second(2)],
    }

    def step(i, _):
        c, f = lax.div(i, FSTEPS), lax.rem(i, FSTEPS)
        for k in range(NCHUNK):
            @pl.when(i == k * FSTEPS)
            def _():
                inward.arrived(k)
                acc[...] = jnp.zeros_like(acc)

        at = pl.multiple_of(f * ftile, ftile)
        h = gelu(dot(fin_i[c].reshape(rows, d_model), win[:, pl.ds(at, ftile)])).astype(BF16)
        acc[...] += dot(h, wout[pl.ds(at, ftile), :])

        for k in range(NCHUNK):
            @pl.when(i == k * FSTEPS + FSTEPS - 1)
            def _():
                put_blocks(hop_r, k, jnp.where(mask[k] > 0.5, acc[...], 0.0))
                back.first(k)
        for at_i, todo in during.items():
            @pl.when(i == at_i)
            def _():
                for fn in todo:
                    fn()
        return 0

    lax.fori_loop(0, NCHUNK * FSTEPS, step, 0)

    combine(1)
    back.third(2)
    back.second(3)
    combine(2)
    back.third(3)
    combine(3)

    inward.drain()
    back.drain()
    sent = vsend.at[pl.ds(1, NDEV - 1)]
    pltpu.make_async_copy(sent, sent, vsend_sem).wait()


def layer(hidden, logits, w_in, w_out):
    tok, d_model = hidden.shape
    n_exp = logits.shape[1]
    ff = w_in.shape[2]
    cols = d_model // NPART
    half = tok // 2

    def path():
        mids = [
            pltpu.VMEM((NCHUNK, *((3, 4) if o[1] < o[0] else (4, 3)), 4, RANKS, cols), BF16) for o in ORDERS
        ]
        return [pltpu.VMEM((NCHUNK, NPART, 7, 4, 4, RANKS, cols), BF16), *mids, pltpu.VMEM((NCHUNK, 4, 4, 4, RANKS, d_model), BF16)]

    n_sem = NCHUNK * NPART * 3
    dma = pltpu.SemaphoreType.DMA
    return pl.pallas_call(
        kernel,
        out_shape=jax.ShapeDtypeStruct(hidden.shape, hidden.dtype),
        in_specs=[pl.BlockSpec(memory_space=pl.ANY)] * 4,
        out_specs=pl.BlockSpec(memory_space=pltpu.VMEM),
        scratch_shapes=[
            pltpu.VMEM((tok, d_model), BF16),
            pltpu.VMEM((tok, n_exp), F32),
            pltpu.VMEM((d_model, ff), BF16),
            pltpu.VMEM((ff, d_model), BF16),
            *path(),
            *path(),
            pltpu.VMEM((2, 512, n_exp), BF16),
            pltpu.VMEM((NCHUNK, 3, half, 512), BF16),
            pltpu.VMEM((NCHUNK, 512, 1), F32),
            pltpu.VMEM((n_exp, n_exp), F32),
            pltpu.VMEM((NDEV, 1, n_exp), F32),
            pltpu.VMEM((NDEV, 1, n_exp), F32),
            pltpu.VMEM((2, half, n_exp), BF16),
            pltpu.VMEM((512, d_model), F32),
            pltpu.VMEM((2, half, d_model), F32),
            dma((4,)),
            dma((n_sem,)),
            dma((n_sem,)),
            dma((n_sem,)),
            dma((n_sem,)),
            dma,
            dma,
        ],
        compiler_params=pltpu.CompilerParams(collective_id=0, has_side_effects=True, vmem_limit_bytes=60 << 20),
    )(hidden, logits, w_in, w_out)


def solution(mesh):
    tok = P(("dp", "ep"), None)
    exp = P("ep", None, None)
    return jax.shard_map(layer, mesh=mesh, in_specs=(tok, tok, exp, exp), out_specs=tok, check_vma=False)
```

time: 201 us -> 99.7 us (0.50)
  Pallas kernels: 0 us -> 97.5 us
  waiting for transfers between devices: 69.4 us -> 0 us
  local copies, waits for them, and re-layouts: 50.2 us -> 2.06 us
  other arithmetic: 37.4 us -> 0 us
  starting transfers between devices: 28.2 us -> 0 us
  matrix products: 14.6 us -> 0 us
    pallas_call x0 -> x1, Pallas kernels: none -> 97.5 us  [layer(): pl.pallas_call(kernel, out_shape=jax.ShapeDtypeStruct(hidden.shape, hidde...]
    all_to_all x3 -> x0, waiting for transfers between devices: 69.4 us -> none  [the longest x1 39.7 us: local_layer(): pool_rows = lax.all_to_all(send_rows, 'ep', 2, 2, tiled=True)]
    gather x7 -> x0, local copies, waits for them, and re-layouts: 33.4 us -> none  [the longest x5 17.2 us: local_layer(): cand_gate = by_owner(jnp.take_along_axis(gate_cols, cand_pos, axis=2))]
    all_to_all x3 -> x0, starting transfers between devices: 28.2 us -> none  [the longest x1 11.5 us: local_layer(): pool_val = lax.all_to_all(by_owner(cand_val), 'ep', 2, 2, tiled=True)]
    scatter-add x1 -> x0, other arithmetic: 15.1 us -> none  [local_layer(): jax.ops.segment_sum(weighted.reshape(-1, d_model), row_ids.reshape(-1), n...]
    dot_general x2 -> x0, matrix products: 14.6 us -> none  [the longest x1 7.55 us: local_layer(): jnp.einsum('emcf,efd->emcd', hidden_act, w_out, preferred_element_type=jn...]
    top_k x2 -> x0, other arithmetic: 11.7 us -> none  [the longest x1 6.95 us: local_layer(): cand_val, cand_pos = lax.top_k(logit_cols, per_src)]
    scatter x1 -> x0, local copies, waits for them, and re-layouts: 7.36 us -> none  [local_layer(): jnp.zeros((local_exp * 2 * pool_len, d_model), jnp.bfloat16).at[flat_ids]]
  transfers between devices with their start and end apart: 3 -> 0, of which waited for: 2 -> 0; matrix products, arithmetic and copies ran while one was open for 18% -> 0% of each run, Pallas kernels for 0% -> 0%
where the time goes in v1:
time: 99.7 us; the launch traced here: 99.6 us
  Pallas kernels  97.5 us (98%)
  local copies, waits for them, and re-layouts  2.06 us (2%)
    pallas_call x1, Pallas kernels, layer(): pl.pallas_call(kernel, out_shape=jax.ShapeDtypeStruct(hidden.shape, hidde...  97.5 us
    unnamed x1, local copies, waits for them, and re-layouts  2.06 us

profile of v1, /device:TPU:1, one launch (start us, length us, event | category | flops | bytes accessed | tf_op | source)
XLA Modules:
  0.0 99.6 jit_solution(10950460979455605029)
XLA Ops:
  0.0 97.5 %shard_map.46 = bf16[512,768]{1,0:T(8,128)(2,1)} custom-call(bf16[512,768]{1,0:T(8,128)(2,1)} %x_hbm.1, f32[512,128]{1,0:T(8,128)} %l_hbm.1, bf16[1,768,3072]{2,1,0:T(8,128)(2,1)} %win_hbm.1, bf16[1,3072,768]{2,1,0:T(8,128)(2,1)} %wout_hbm.1), custom_call_target="tpu_custom_call" | custom-call | tf_op jit(solution)/shard_map/pallas_call | solution.py:377
  97.5 2.1 %copy.6 = bf16[512,768]{1,0:T(8,128)(2,1)} copy(bf16[512,768]{1,0:T(8,128)(2,1)} %shard_map.46) | data formatting | bytes 1572864

commit v2 on v1

--- a/solution.py
+++ b/solution.py
@@ -139,11 +139,14 @@
             self.wait_recv(c, p, 1)
             self.send2(c, p)
 
+    def arrived_part(self, c, p):
+        self.wait_recv(c, p, 2)
+        if c % 2 == 0:
+            self.own(c, p)
+
     def arrived(self, c):
         for p in range(NPART):
-            self.wait_recv(c, p, 2)
-            if c % 2 == 0:
-                self.own(c, p)
+            self.arrived_part(c, p)
 
     def drain(self):
         for c in range(NCHUNK):
@@ -155,8 +158,8 @@
 def kernel(
     x_hbm, l_hbm, win_hbm, wout_hbm, out_ref,
     x_ref, l_ref, win, wout, hop_i, mid_i0, mid_i1, mid_i2, fin_i, hop_r, mid_r0, mid_r1, mid_r2, fin_r,
-    place, comb, mask, tops, vsend, vrecv, rank, acc, yacc,
-    load_sem, send_i, recv_i, send_r, recv_r, vsend_sem, vrecv_sem,
+    place, comb, mask, tops, tell_hop, tell_mid, told, rank, acc, yacc,
+    load_sem, send_i, recv_i, send_r, recv_r, tell_send, tell_recv,
 ):
     me = lax.axis_index("ep")
     half, n_exp = l_ref.shape[0] // 2, l_ref.shape[1]
@@ -174,14 +177,12 @@
 
     barrier = pltpu.get_barrier_semaphore()
 
-    def hello(k, _):
-        pl.semaphore_signal(barrier, inc=1, device_id=(0, lax.rem(me + k, NDEV)), device_id_type=MESH)
-        return 0
-
-    lax.fori_loop(1, NDEV, hello, 0)
-
     inward = Exchange(me, 1, hop_i, (mid_i0, mid_i1, mid_i2), fin_i, send_i, recv_i, cols)
     back = Exchange(me, -1, hop_r, (mid_r0, mid_r1, mid_r2), fin_r, send_r, recv_r, cols)
+
+    peers = [inward.peers[dim, d, core] for core in range(2) for dim in range(3) for d in (1, 2, 3)] + [inward.peers[0, 0, 1]]
+    for to in peers:
+        pl.semaphore_signal(barrier, inc=1, device_id=(0, to), device_id_type=MESH)
 
     pos = coords(me)
     for core in range(2):
@@ -205,9 +206,7 @@
                 dst[c, 1, (y + 3) % 4, z] = p1
                 dst[c, 2, (z + 3) % 4, :, y] = p2
 
-    loads[0].wait()
-    tops[...] = jnp.zeros_like(tops)
-    for m in range(2):
+    def select(m):
         cur = l_ref[m * half : (m + 1) * half, :]
         rk = jnp.full(cur.shape, 15.0, F32)
         for r in range(RANKS):
@@ -215,109 +214,140 @@
             hit = cur == top
             rk = jnp.where(hit, float(r), rk)
             cur = jnp.where(hit, -1e30, cur)
-            tops[m * RANKS + r : m * RANKS + r + 1, :] = top
+            for g in range(8):
+                at = g * 16 + m * RANKS + r
+                tops[at : at + 1, :] = top
         rank[m] = rk.astype(BF16)
-        if m == 0:
-            loads[1].wait()
+
+    def gather(c):
+        m, core = c // 2, c % 2
+        wide = dot_t(place[core], rank[m])
+        r_of = (lax.broadcasted_iota(jnp.int32, wide.shape, 0) & 7).astype(F32)
+        pick = jnp.where(wide == r_of, 1.0, 0.0).astype(BF16)
+        put_blocks(hop_i, c, dot(pick, x_ref[m * half : (m + 1) * half, :]))
+
+    def tell_copy(src, dst, phase, dim, d, core):
+        pltpu.make_async_remote_copy(
+            src, dst, tell_send.at[phase], tell_recv.at[phase], device_id=(0, inward.peers[dim, d, core]), device_id_type=MESH
+        ).start()
+
+    def tell_wait(sem, phase, ref):
+        pltpu.make_async_copy(ref, ref, sem.at[phase]).wait()
+
+    def tell_first():
+        q = lax.broadcasted_iota(jnp.int32, (NDEV, n_exp), 0)
+        e = lax.broadcasted_iota(jnp.int32, (NDEV, n_exp), 1)
+        ex = ((q >> 5) + 1 + pos[2]) & 3
+        ey = ((q >> 3) + pos[1]) & 3
+        ez = ((q >> 1) + pos[0]) & 3
+        ec = (q + pos[3]) & 1
+        at = jnp.where(e == ez * 32 + ey * 8 + ex * 2 + ec, 1.0, 0.0).astype(BF16)
+        hi, mid, low = (dot_t(at, v) for v in split3(tops[...]))
+        tell_hop[0:4] = ((hi + mid) + low).reshape(4, 4, 4, 2, 1, n_exp)
+        for d in (1, 3, 2):
+            tell_copy(tell_hop.at[d - 1], tell_hop.at[3 + d], 0, 2, d, 0)
+
+    def tell_second():
+        tell_wait(tell_recv, 0, tell_hop.at[pl.ds(4, 3)])
+        for d in (1, 3, 2):
+            tell_copy(tell_hop.at[pl.ds(3, 4), d], tell_mid.at[d - 1], 1, 1, d, 0)
+
+    def tell_third():
+        tell_wait(tell_recv, 1, tell_mid)
         for core in range(2):
-            wide = dot_t(place[core], rank[m])
-            r_of = (lax.broadcasted_iota(jnp.int32, wide.shape, 0) & 7).astype(F32)
-            pick = jnp.where(wide == r_of, 1.0, 0.0).astype(BF16)
-            put_blocks(hop_i, m * 2 + core, dot(pick, x_ref[m * half : (m + 1) * half, :]))
-        if m == 0:
-            pl.semaphore_wait(barrier, NDEV - 1)
-            inward.first(0)
-            inward.first(1)
-
-    eye = jnp.where(
-        lax.broadcasted_iota(jnp.int32, (n_exp, n_exp), 0) == lax.broadcasted_iota(jnp.int32, (n_exp, n_exp), 1), 1.0, 0.0
-    ).astype(BF16)
-    hi, mid, low = (dot_t(eye, v) for v in split3(tops[...]))
-    vsend[...] = ((hi + mid) + low).reshape(n_exp, 1, n_exp)
-
+            for d in (1, 3, 2, 0):
+                if core or d:
+                    tell_copy(tell_hop.at[pl.ds(3, 4), 0, d, core], told.at[core, d, 0], 3 - core, 0, d, core)
+                    tell_copy(tell_mid.at[:, :, d, core], told.at[core, d, pl.ds(1, 3)], 3 - core, 0, d, core)
+
+    def owner_cut():
+        for ref, sem in ((told.at[1], tell_recv.at[2]), (told.at[0, pl.ds(1, 3)], tell_recv.at[3])):
+            pltpu.make_async_copy(ref, ref, sem).wait()
+        told[0, 0, 0] = tell_hop[3:7, 0, 0, 0]
+        told[0, 0, 1:4] = tell_mid[:, :, 0, 0]
+        seen = told[...].reshape(NDEV, n_exp)
+        lane = lax.broadcasted_iota(jnp.int32, (n_exp, n_exp), 1)
+        row = lax.broadcasted_iota(jnp.int32, (n_exp, n_exp), 0)
+        same = jnp.where((lane >> 3) == (row >> 3), 1.0, 0.0).astype(BF16)
+        first = jnp.where(((row & 7) == 0) & (((lane >> 3) & 1) == ((row >> 3) & 1)), 1.0, 0.0).astype(BF16)
+        group = (lax.broadcasted_iota(jnp.int32, (8, n_exp), 1) >> 4).astype(F32)
+        base = jnp.full((8, n_exp), -8.0, F32)
+        width = 2.0
+        for _ in range(8):
+            cand = base + group * width
+            over = jnp.where(seen >= cand[0:1], 1.0, 0.0)
+            cnt = jnp.sum(over, axis=0, keepdims=True)
+            cnt = dot(jnp.broadcast_to(cnt, (8, n_exp)).astype(BF16), same)
+            flag = jnp.where(cnt >= float(KEEP), 1.0, 0.0).astype(BF16)
+            base = base + (dot(flag, first) - 1.0) * width
+            width = width / 8.0
+        chosen = jnp.where(seen >= base[0:1], 1.0, 0.0).astype(BF16)
+        for core in range(2):
+            q = lax.broadcasted_iota(jnp.int32, (rows, NDEV), 0)
+            src = lax.broadcasted_iota(jnp.int32, (rows, NDEV), 1)
+            wide = dot(jnp.where(src == (q >> 3) + core * 64, 1.0, 0.0).astype(BF16), chosen)
+            for m in range(2):
+                keep = jnp.where(src == (q & 7) + m * 8, wide, 0.0)
+                mask[m * 2 + core] = jnp.sum(keep, axis=1, keepdims=True)
+
+    def gates():
+        for m in range(2):
+            lg = l_ref[m * half : (m + 1) * half, :]
+            ex = jnp.exp(lg - jnp.max(lg, axis=1, keepdims=True))
+            terms = split3(ex / jnp.sum(ex, axis=1, keepdims=True))
+            for core in range(2):
+                wide = dot_t(rank[m], place[core])
+                r_of = (lax.broadcasted_iota(jnp.int32, wide.shape, 1) & 7).astype(F32)
+                hit = wide == r_of
+                for i, term in enumerate(terms):
+                    comb[m * 2 + core, i] = jnp.where(hit, dot_t(term, place[core]), 0.0).astype(BF16)
+
+    def combine(c):
+        m, core = c // 2, c % 2
+        for p in range(NPART):
+            back.arrived_part(c, p)
+            at = slice(p * cols, (p + 1) * cols)
+            y = fin_r[c, :, :, :, :, at].reshape(rows, cols)
+            total = dot(comb[c, 0], y) + dot(comb[c, 1], y) + dot(comb[c, 2], y)
+            if core == 0:
+                yacc[m, :, at] = total
+            else:
+                both = x_ref[m * half : (m + 1) * half, at].astype(F32) + (yacc[m, :, at] + total)
+                out_ref[m * half : (m + 1) * half, at] = both.astype(BF16)
+
+    loads[0].wait()
+    tops[...] = jnp.zeros_like(tops)
+    select(0)
+    loads[1].wait()
+    gather(0)
+    pl.semaphore_wait(barrier, len(peers))
+    inward.first(0)
+    gather(1)
+    inward.first(1)
+    select(1)
+    tell_first()
+    gather(2)
+    gather(3)
+    inward.first(3)
+    gates()
     inward.second(0)
+    tell_second()
     inward.first(2)
-
-    def tell(k, _):
-        kz, ky, kx, kc = coords(k)
-        to = shifted(me, (kz, ky, kx), kc)
-        pltpu.make_async_remote_copy(
-            vsend.at[to], vrecv.at[k], vsend_sem, vrecv_sem, device_id=(0, to), device_id_type=MESH
-        ).start()
-        return 0
-
-    lax.fori_loop(1, NDEV, tell, 0)
-    vrecv[0] = vsend[me]
-
     inward.second(1)
-
-    for m in range(2):
-        lg = l_ref[m * half : (m + 1) * half, :]
-        ex = jnp.exp(lg - jnp.max(lg, axis=1, keepdims=True))
-        terms = split3(ex / jnp.sum(ex, axis=1, keepdims=True))
-        for core in range(2):
-            wide = dot_t(rank[m], place[core])
-            r_of = (lax.broadcasted_iota(jnp.int32, wide.shape, 1) & 7).astype(F32)
-            hit = wide == r_of
-            for i, term in enumerate(terms):
-                comb[m * 2 + core, i] = jnp.where(hit, dot_t(term, place[core]), 0.0).astype(BF16)
-        if m == 0:
-            inward.third(0)
-            inward.first(3)
-
+    tell_third()
+    inward.third(0)
+    owner_cut()
     inward.second(2)
-
-    told = vrecv.at[pl.ds(1, NDEV - 1)]
-    pltpu.make_async_copy(told, told, vrecv_sem).wait()
-    seen = vrecv[...].reshape(NDEV, n_exp)
-    lane = lax.broadcasted_iota(jnp.int32, (NDEV, n_exp), 1)
-    cut = None
-    for m in range(2):
-        mine = (lane >> 3) == m
-
-        def bisect(_, state):
-            low_end, width = state
-            cand = low_end + width
-            cnt = jnp.sum(jnp.where(mine & (seen >= cand), 1.0, 0.0), axis=0, keepdims=True)
-            cnt = jnp.sum(cnt, axis=1, keepdims=True)
-            return jnp.where(cnt >= float(KEEP), cand, low_end), width * 0.5
-
-        t = lax.fori_loop(0, 24, bisect, (jnp.full((1, 1), -8.0, F32), jnp.full((1, 1), 8.0, F32)))[0]
-        cut = t if m == 0 else jnp.where((lane >> 3) == 0, cut, t)
-    chosen = jnp.where(seen >= cut, 1.0, 0.0).astype(BF16)
-    for core in range(2):
-        q = lax.broadcasted_iota(jnp.int32, (rows, NDEV), 0)
-        src = lax.broadcasted_iota(jnp.int32, (rows, NDEV), 1)
-        wide = dot(jnp.where(src == (q >> 3) * 2 + core, 1.0, 0.0).astype(BF16), chosen)
-        for m in range(2):
-            keep = jnp.where(src == (q & 7) + m * 8, wide, 0.0)
-            mask[m * 2 + core] = jnp.sum(keep, axis=1, keepdims=True)
-
     inward.third(1)
     loads[2].wait()
     loads[3].wait()
-
-    def combine(c):
-        back.arrived(c)
-        m, core = c // 2, c % 2
-        y = fin_r[c].reshape(rows, d_model)
-        total = dot(comb[c, 0], y) + dot(comb[c, 1], y) + dot(comb[c, 2], y)
-        if core == 0:
-            yacc[m] = total
-        else:
-            both = x_ref[m * half : (m + 1) * half, :].astype(F32) + (yacc[m] + total)
-            out_ref[m * half : (m + 1) * half, :] = both.astype(BF16)
 
     during = {
         1: [lambda: inward.second(3)],
         3: [lambda: inward.third(2)],
         7: [lambda: inward.third(3)],
-        12: [lambda: back.second(0)],
-        15: [lambda: back.second(1)],
-        17: [lambda: back.third(0)],
-        19: [lambda: back.third(1)],
-        21: [lambda: combine(0)],
-        22: [lambda: back.second(2)],
+        14: [lambda: back.second(0)],
+        18: [lambda: back.second(1)],
     }
 
     def step(i, _):
@@ -346,17 +376,23 @@
 
     lax.fori_loop(0, NCHUNK * FSTEPS, step, 0)
 
+    back.second(2)
+    back.third(0)
+    back.second(3)
+    back.third(2)
+    back.third(1)
+    back.third(3)
+    combine(0)
     combine(1)
-    back.third(2)
-    back.second(3)
     combine(2)
-    back.third(3)
     combine(3)
 
     inward.drain()
     back.drain()
-    sent = vsend.at[pl.ds(1, NDEV - 1)]
-    pltpu.make_async_copy(sent, sent, vsend_sem).wait()
+    tell_wait(tell_send, 0, tell_hop.at[pl.ds(4, 3)])
+    tell_wait(tell_send, 1, tell_mid)
+    for ref, sem in ((told.at[1], tell_send.at[2]), (told.at[0, pl.ds(1, 3)], tell_send.at[3])):
+        pltpu.make_async_copy(ref, ref, sem).wait()
 
 
 def layer(hidden, logits, w_in, w_out):
@@ -390,8 +426,9 @@
             pltpu.VMEM((NCHUNK, 3, half, 512), BF16),
             pltpu.VMEM((NCHUNK, 512, 1), F32),
             pltpu.VMEM((n_exp, n_exp), F32),
-            pltpu.VMEM((NDEV, 1, n_exp), F32),
-            pltpu.VMEM((NDEV, 1, n_exp), F32),
+            pltpu.VMEM((7, 4, 4, 2, 1, n_exp), F32),
+            pltpu.VMEM((3, 4, 4, 2, 1, n_exp), F32),
+            pltpu.VMEM((2, 4, 4, 4, 1, n_exp), F32),
             pltpu.VMEM((2, half, n_exp), BF16),
             pltpu.VMEM((512, d_model), F32),
             pltpu.VMEM((2, half, d_model), F32),
@@ -400,8 +437,8 @@
             dma((n_sem,)),
             dma((n_sem,)),
             dma((n_sem,)),
-            dma,
-            dma,
+            dma((4,)),
+            dma((4,)),
         ],
         compiler_params=pltpu.CompilerParams(collective_id=0, has_side_effects=True, vmem_limit_bytes=60 << 20),
     )(hidden, logits, w_in, w_out)

time: 99.7 us -> 92.8 us (0.931)
  Pallas kernels: 97.5 us -> 90.6 us
    pallas_call x1, Pallas kernels: 97.5 us -> 90.6 us  [layer(): pl.pallas_call(kernel, out_shape=jax.ShapeDtypeStruct(hidden.shape, hidde...]
where the time goes in v2:
time: 92.8 us; the launch traced here: 92.7 us
  Pallas kernels  90.6 us (98%)
  local copies, waits for them, and re-layouts  2.06 us (2%)
    pallas_call x1, Pallas kernels, layer(): pl.pallas_call(kernel, out_shape=jax.ShapeDtypeStruct(hidden.shape, hidde...  90.6 us
    unnamed x1, local copies, waits for them, and re-layouts  2.06 us

profile of v2, /device:TPU:1, one launch (start us, length us, event | category | flops | bytes accessed | tf_op | source)
XLA Modules:
  0.0 92.7 jit_solution(10868948082763154737)
XLA Ops:
  0.0 90.6 %shard_map.46 = bf16[512,768]{1,0:T(8,128)(2,1)} custom-call(bf16[512,768]{1,0:T(8,128)(2,1)} %x_hbm.1, f32[512,128]{1,0:T(8,128)} %l_hbm.1, bf16[1,768,3072]{2,1,0:T(8,128)(2,1)} %win_hbm.1, bf16[1,3072,768]{2,1,0:T(8,128)(2,1)} %wout_hbm.1), custom_call_target="tpu_custom_call" | custom-call | tf_op jit(solution)/shard_map/pallas_call | solution.py:413
  90.6 2.1 %copy.6 = bf16[512,768]{1,0:T(8,128)(2,1)} copy(bf16[512,768]{1,0:T(8,128)(2,1)} %shard_map.46) | data formatting | bytes 1572864

commit v3 on v2

--- a/solution.py
+++ b/solution.py
@@ -315,6 +315,10 @@
                 both = x_ref[m * half : (m + 1) * half, at].astype(F32) + (yacc[m, :, at] + total)
                 out_ref[m * half : (m + 1) * half, at] = both.astype(BF16)
 
+    def more():
+        gather(2)
+        gather(3)
+
     loads[0].wait()
     tops[...] = jnp.zeros_like(tops)
     select(0)
@@ -322,32 +326,31 @@
     gather(0)
     pl.semaphore_wait(barrier, len(peers))
     inward.first(0)
+    select(1)
+    tell_first()
     gather(1)
     inward.first(1)
-    select(1)
-    tell_first()
-    gather(2)
-    gather(3)
+    inward.second(0)
+    inward.second(1)
+    more()
+    tell_second()
+    inward.third(0)
+    inward.first(2)
+    tell_third()
     inward.first(3)
-    gates()
-    inward.second(0)
-    tell_second()
-    inward.first(2)
-    inward.second(1)
-    tell_third()
-    inward.third(0)
-    owner_cut()
-    inward.second(2)
     inward.third(1)
     loads[2].wait()
     loads[3].wait()
 
     during = {
-        1: [lambda: inward.second(3)],
-        3: [lambda: inward.third(2)],
-        7: [lambda: inward.third(3)],
-        14: [lambda: back.second(0)],
-        18: [lambda: back.second(1)],
+        2: [lambda: inward.second(2), lambda: owner_cut()],
+        4: [lambda: inward.second(3)],
+        7: [lambda: inward.third(2)],
+        11: [lambda: inward.third(3)],
+        12: [lambda: back.second(0)],
+        15: [lambda: back.second(1)],
+        18: [lambda: back.third(0)],
+        20: [lambda: back.third(1)],
     }
 
     def step(i, _):
@@ -377,10 +380,9 @@
     lax.fori_loop(0, NCHUNK * FSTEPS, step, 0)
 
     back.second(2)
-    back.third(0)
     back.second(3)
+    gates()
     back.third(2)
-    back.third(1)
     back.third(3)
     combine(0)
     combine(1)

time: 92.8 us -> 87.4 us (0.942)
  Pallas kernels: 90.6 us -> 85.2 us
    pallas_call x1, Pallas kernels: 90.6 us -> 85.2 us  [layer(): pl.pallas_call(kernel, out_shape=jax.ShapeDtypeStruct(hidden.shape, hidde...]
where the time goes in v3:
time: 87.4 us; the launch traced here: 87.3 us
  Pallas kernels  85.2 us (97%)
  local copies, waits for them, and re-layouts  2.06 us (2%)
    pallas_call x1, Pallas kernels, layer(): pl.pallas_call(kernel, out_shape=jax.ShapeDtypeStruct(hidden.shape, hidde...  85.2 us
    unnamed x1, local copies, waits for them, and re-layouts  2.06 us

profile of v3, /device:TPU:1, one launch (start us, length us, event | category | flops | bytes accessed | tf_op | source)
XLA Modules:
  0.0 87.3 jit_solution(8321037473043133379)
XLA Ops:
  0.0 85.2 %shard_map.46 = bf16[512,768]{1,0:T(8,128)(2,1)} custom-call(bf16[512,768]{1,0:T(8,128)(2,1)} %x_hbm.1, f32[512,128]{1,0:T(8,128)} %l_hbm.1, bf16[1,768,3072]{2,1,0:T(8,128)(2,1)} %win_hbm.1, bf16[1,3072,768]{2,1,0:T(8,128)(2,1)} %wout_hbm.1), custom_call_target="tpu_custom_call" | custom-call | tf_op jit(solution)/shard_map/pallas_call | solution.py:415
  85.2 2.1 %copy.6 = bf16[512,768]{1,0:T(8,128)(2,1)} copy(bf16[512,768]{1,0:T(8,128)(2,1)} %shard_map.46) | data formatting | bytes 1572864

commit v4 on v3

--- a/solution.py
+++ b/solution.py
@@ -156,8 +156,8 @@
 
 
 def kernel(
-    x_hbm, l_hbm, win_hbm, wout_hbm, out_ref,
-    x_ref, l_ref, win, wout, hop_i, mid_i0, mid_i1, mid_i2, fin_i, hop_r, mid_r0, mid_r1, mid_r2, fin_r,
+    x_ref, l_ref, win_hbm, wout_hbm, out_ref,
+    win, wout, hop_i, mid_i0, mid_i1, mid_i2, fin_i, hop_r, mid_r0, mid_r1, mid_r2, fin_r,
     place, comb, mask, tops, tell_hop, tell_mid, told, rank, acc, yacc,
     load_sem, send_i, recv_i, send_r, recv_r, tell_send, tell_recv,
 ):
@@ -170,7 +170,7 @@
 
     loads = [
         pltpu.make_async_copy(s, d, load_sem.at[i])
-        for i, (s, d) in enumerate(((l_hbm, l_ref), (x_hbm, x_ref), (win_hbm.at[0], win), (wout_hbm.at[0], wout)))
+        for i, (s, d) in enumerate(((win_hbm.at[0], win), (wout_hbm.at[0], wout)))
     ]
     for ld in loads:
         ld.start()
@@ -319,10 +319,8 @@
         gather(2)
         gather(3)
 
-    loads[0].wait()
     tops[...] = jnp.zeros_like(tops)
     select(0)
-    loads[1].wait()
     gather(0)
     pl.semaphore_wait(barrier, len(peers))
     inward.first(0)
@@ -339,8 +337,8 @@
     tell_third()
     inward.first(3)
     inward.third(1)
-    loads[2].wait()
-    loads[3].wait()
+    loads[0].wait()
+    loads[1].wait()
 
     during = {
         2: [lambda: inward.second(2), lambda: owner_cut()],
@@ -415,11 +413,9 @@
     return pl.pallas_call(
         kernel,
         out_shape=jax.ShapeDtypeStruct(hidden.shape, hidden.dtype),
-        in_specs=[pl.BlockSpec(memory_space=pl.ANY)] * 4,
+        in_specs=[pl.BlockSpec(memory_space=pltpu.VMEM)] * 2 + [pl.BlockSpec(memory_space=pl.ANY)] * 2,
         out_specs=pl.BlockSpec(memory_space=pltpu.VMEM),
         scratch_shapes=[
-            pltpu.VMEM((tok, d_model), BF16),
-            pltpu.VMEM((tok, n_exp), F32),
             pltpu.VMEM((d_model, ff), BF16),
             pltpu.VMEM((ff, d_model), BF16),
             *path(),
@@ -434,7 +430,7 @@
             pltpu.VMEM((2, half, n_exp), BF16),
             pltpu.VMEM((512, d_model), F32),
             pltpu.VMEM((2, half, d_model), F32),
-            dma((4,)),
+            dma((2,)),
             dma((n_sem,)),
             dma((n_sem,)),
             dma((n_sem,)),
@@ -442,7 +438,7 @@
             dma((4,)),
             dma((4,)),
         ],
-        compiler_params=pltpu.CompilerParams(collective_id=0, has_side_effects=True, vmem_limit_bytes=60 << 20),
+        compiler_params=pltpu.CompilerParams(collective_id=0, has_side_effects=True, vmem_limit_bytes=52 << 20),
     )(hidden, logits, w_in, w_out)
 
 

time: 87.4 us -> 87.3 us (level)
  Pallas kernels: 85.2 us -> 84.2 us
  local copies, waits for them, and re-layouts: 2.06 us -> 2.96 us
    pallas_call x1, Pallas kernels: 85.2 us -> 84.2 us  [layer(): pl.pallas_call(kernel, out_shape=jax.ShapeDtypeStruct(hidden.shape, hidde...]
    unnamed x1 -> x5, local copies, waits for them, and re-layouts: 2.06 us -> 2.96 us
where the time goes in v4:
time: 87.3 us; the launch traced here: 87.2 us
  Pallas kernels  84.2 us (96%)
  local copies, waits for them, and re-layouts  2.96 us (3%)
    pallas_call x1, Pallas kernels, layer(): pl.pallas_call(kernel, out_shape=jax.ShapeDtypeStruct(hidden.shape, hidde...  84.2 us
    unnamed x5, local copies, waits for them, and re-layouts  2.96 us

profile of v4, /device:TPU:1, one launch (start us, length us, event | category | flops | bytes accessed | tf_op | source)
XLA Modules:
  0.0 87.2 jit_solution(11091688922900935007)
XLA Ops:
  0.0 0.0 copy-start
  0.0 1.1 %copy-done = bf16[512,768]{1,0:T(8,128)(2,1)S(1)} copy-done((bf16[512,768]{1,0:T(8,128)(2,1)S(1)}, bf16[512,768]{1,0:T(8,128)(2,1)}, u32[]{:S(2)}) %copy-start) | copy-done | bytes 786456
  1.1 0.0 copy-start.1
  1.1 0.9 %copy-done.1 = f32[512,128]{1,0:T(8,128)S(1)} copy-done((f32[512,128]{1,0:T(8,128)S(1)}, f32[512,128]{1,0:T(8,128)}, u32[]{:S(2)}) %copy-start.1) | copy-done | bytes 262168
  2.1 84.2 %shard_map.46 = bf16[512,768]{1,0:T(8,128)(2,1)S(1)} custom-call(bf16[512,768]{1,0:T(8,128)(2,1)S(1)} %copy-done, f32[512,128]{1,0:T(8,128)S(1)} %copy-done.1, bf16[1,768,3072]{2,1,0:T(8,128)(2,1)} %win_hbm.1, bf16[1,3072,768]{2,1,0:T(8,128)(2,1)} %wout_hbm.1), custom_call_target="tpu_custom_call" | custom-call | tf_op jit(solution)/shard_map/pallas_call | solution.py:413
  86.3 0.9 %copy.6 = bf16[512,768]{1,0:T(8,128)(2,1)} copy(bf16[512,768]{1,0:T(8,128)(2,1)S(1)} %shard_map.46) | data formatting | bytes 1572864
Async XLA Ops:
  0.0 1.1 %copy-start = (bf16[512,768]{1,0:T(8,128)(2,1)S(1)}, bf16[512,768]{1,0:T(8,128)(2,1)}, u32[]{:S(2)}) copy-start(bf16[512,768]{1,0:T(8,128)(2,1)} %x_ref.1) | copy-start | bytes 2359300
  1.1 0.9 %copy-start.1 = (f32[512,128]{1,0:T(8,128)S(1)}, f32[512,128]{1,0:T(8,128)}, u32[]{:S(2)}) copy-start(f32[512,128]{1,0:T(8,128)} %l_ref.1) | copy-start | bytes 786436

commit v5 on v3

--- a/solution.py
+++ b/solution.py
@@ -442,8 +442,8 @@
             dma((4,)),
             dma((4,)),
         ],
-        compiler_params=pltpu.CompilerParams(collective_id=0, has_side_effects=True, vmem_limit_bytes=60 << 20),
-    )(hidden, logits, w_in, w_out)
+        compiler_params=pltpu.CompilerParams(collective_id=0, has_side_effects=True, vmem_limit_bytes=52 << 20),
+    )(pltpu.with_memory_space_constraint(hidden, pltpu.HBM), pltpu.with_memory_space_constraint(logits, pltpu.HBM), w_in, w_out)
 
 
 def solution(mesh):

time: 87.4 us -> 85.3 us (0.976)
  local copies, waits for them, and re-layouts: 2.06 us -> 0.88 us
  Pallas kernels: 85.2 us -> 84.3 us
    unnamed x1, local copies, waits for them, and re-layouts: 2.06 us -> 0.88 us
where the time goes in v5:
time: 85.3 us; the launch traced here: 85.2 us
  Pallas kernels  84.3 us (99%)
  local copies, waits for them, and re-layouts  0.88 us (1%)
    pallas_call x1, Pallas kernels, layer(): pl.pallas_call(kernel, out_shape=jax.ShapeDtypeStruct(hidden.shape, hidde...  84.3 us

profile of v5, /device:TPU:1, one launch (start us, length us, event | category | flops | bytes accessed | tf_op | source)
XLA Modules:
  0.0 85.2 jit_solution(6252654323193934116)
XLA Ops:
  0.0 84.3 %shard_map.46 = bf16[512,768]{1,0:T(8,128)(2,1)S(1)} custom-call(bf16[512,768]{1,0:T(8,128)(2,1)} %x_hbm.1, f32[512,128]{1,0:T(8,128)} %l_hbm.1, bf16[1,768,3072]{2,1,0:T(8,128)(2,1)} %win_hbm.1, bf16[1,3072,768]{2,1,0:T(8,128)(2,1)} %wout_hbm.1), custom_call_target="tpu_custom_call" | custom-call | tf_op jit(solution)/shard_map/pallas_call | solution.py:415
  84.3 0.9 %copy.6 = bf16[512,768]{1,0:T(8,128)(2,1)} copy(bf16[512,768]{1,0:T(8,128)(2,1)S(1)} %shard_map.46) | data formatting | bytes 1572864

commit v6 on v5

--- a/solution.py
+++ b/solution.py
@@ -16,7 +16,7 @@
 ORDERS = ((2, 1, 0), (1, 0, 2), (0, 2, 1))
 NPART = 3
 NCHUNK = 4
-FSTEPS = 6
+FSTEPS = 3
 
 
 def coords(d):
@@ -148,10 +148,10 @@
         for p in range(NPART):
             self.arrived_part(c, p)
 
-    def drain(self):
-        for c in range(NCHUNK):
+    def drain(self, chunks, phases=(0, 1, 2)):
+        for c in chunks:
             for p in range(NPART):
-                for phase in range(3):
+                for phase in phases:
                     self.wait_send(c, p, phase)
 
 
@@ -302,8 +302,20 @@
                 for i, term in enumerate(terms):
                     comb[m * 2 + core, i] = jnp.where(hit, dot_t(term, place[core]), 0.0).astype(BF16)
 
+    def drain_early():
+        inward.drain(range(NCHUNK))
+        tell_wait(tell_send, 0, tell_hop.at[pl.ds(4, 3)])
+        tell_wait(tell_send, 1, tell_mid)
+        for ref, sem in ((told.at[1], tell_send.at[2]), (told.at[0, pl.ds(1, 3)], tell_send.at[3])):
+            pltpu.make_async_copy(ref, ref, sem).wait()
+
     def combine(c):
         m, core = c // 2, c % 2
+        if c == 2:
+            drain_early()
+        if c == 3:
+            back.drain(range(3))
+            back.drain((3,), (0, 1))
         for p in range(NPART):
             back.arrived_part(c, p)
             at = slice(p * cols, (p + 1) * cols)
@@ -330,27 +342,26 @@
     tell_first()
     gather(1)
     inward.first(1)
+    more()
+    inward.first(3)
+    tell_second()
     inward.second(0)
+    inward.first(2)
     inward.second(1)
-    more()
-    tell_second()
+    tell_third()
     inward.third(0)
-    inward.first(2)
-    tell_third()
-    inward.first(3)
+    inward.second(2)
     inward.third(1)
+    inward.second(3)
+    owner_cut()
     loads[2].wait()
     loads[3].wait()
 
     during = {
-        2: [lambda: inward.second(2), lambda: owner_cut()],
-        4: [lambda: inward.second(3)],
-        7: [lambda: inward.third(2)],
-        11: [lambda: inward.third(3)],
-        12: [lambda: back.second(0)],
-        15: [lambda: back.second(1)],
-        18: [lambda: back.third(0)],
-        20: [lambda: back.third(1)],
+        1: [lambda: inward.third(2)],
+        4: [lambda: inward.third(3)],
+        7: [lambda: back.second(0)],
+        9: [lambda: back.second(1)],
     }
 
     def step(i, _):
@@ -379,22 +390,19 @@
 
     lax.fori_loop(0, NCHUNK * FSTEPS, step, 0)
 
+    back.third(0)
     back.second(2)
+    gates()
     back.second(3)
-    gates()
+    back.third(1)
+    combine(0)
     back.third(2)
     back.third(3)
-    combine(0)
     combine(1)
     combine(2)
     combine(3)
 
-    inward.drain()
-    back.drain()
-    tell_wait(tell_send, 0, tell_hop.at[pl.ds(4, 3)])
-    tell_wait(tell_send, 1, tell_mid)
-    for ref, sem in ((told.at[1], tell_send.at[2]), (told.at[0, pl.ds(1, 3)], tell_send.at[3])):
-        pltpu.make_async_copy(ref, ref, sem).wait()
+    back.drain((3,), (2,))
 
 
 def layer(hidden, logits, w_in, w_out):

time: 85.3 us -> 83 us (0.973)
  Pallas kernels: 84.3 us -> 82 us
    pallas_call x1, Pallas kernels: 84.3 us -> 82 us  [layer(): pl.pallas_call(kernel, out_shape=jax.ShapeDtypeStruct(hidden.shape, hidde...]
where the time goes in v6:
time: 83 us; the launch traced here: 82.9 us
  Pallas kernels  82 us (99%)
  local copies, waits for them, and re-layouts  0.88 us (1%)
    pallas_call x1, Pallas kernels, layer(): pl.pallas_call(kernel, out_shape=jax.ShapeDtypeStruct(hidden.shape, hidde...  82 us

profile of v6, /device:TPU:1, one launch (start us, length us, event | category | flops | bytes accessed | tf_op | source)
XLA Modules:
  0.0 82.9 jit_solution(13392704673739115873)
XLA Ops:
  0.0 82.0 %shard_map.46 = bf16[512,768]{1,0:T(8,128)(2,1)S(1)} custom-call(bf16[512,768]{1,0:T(8,128)(2,1)} %x_hbm.1, f32[512,128]{1,0:T(8,128)} %l_hbm.1, bf16[1,768,3072]{2,1,0:T(8,128)(2,1)} %win_hbm.1, bf16[1,3072,768]{2,1,0:T(8,128)(2,1)} %wout_hbm.1), custom_call_target="tpu_custom_call" | custom-call | tf_op jit(solution)/shard_map/pallas_call | solution.py:423
  82.0 0.9 %copy.6 = bf16[512,768]{1,0:T(8,128)(2,1)} copy(bf16[512,768]{1,0:T(8,128)(2,1)S(1)} %shard_map.46) | data formatting | bytes 1572864

commit v7 on v6

--- a/solution.py
+++ b/solution.py
@@ -86,16 +86,16 @@
         return self.final.at[(c, *idx, slice(None), pl.ds(p * self.cols, self.cols))]
 
     def send0(self, c, p):
-        for d in (1, 3, 2):
+        for d in (2, 1, 3):
             self.copy(self.hop.at[c, p, d - 1], self.hop.at[c, p, 3 + d], c, p, 0, d, 0)
 
     def send1(self, c, p):
-        for d in (1, 3, 2):
+        for d in (2, 1, 3):
             self.copy(self.hop.at[c, p, pl.ds(3, 4), d], self.mid_at(p, c, d), c, p, 1, d, 0)
 
     def send2(self, c, p):
         core = c % 2
-        for d in (1, 3, 2, 0):
+        for d in (2, 1, 3, 0):
             if d == 0 and core == 0:
                 continue
             self.copy(self.hop.at[c, p, pl.ds(3, 4), 0, d], self.final_at(c, p, (pl.ds(0, 4), 0, d)), c, p, 2, d, core)
@@ -244,18 +244,18 @@
         at = jnp.where(e == ez * 32 + ey * 8 + ex * 2 + ec, 1.0, 0.0).astype(BF16)
         hi, mid, low = (dot_t(at, v) for v in split3(tops[...]))
         tell_hop[0:4] = ((hi + mid) + low).reshape(4, 4, 4, 2, 1, n_exp)
-        for d in (1, 3, 2):
+        for d in (2, 1, 3):
             tell_copy(tell_hop.at[d - 1], tell_hop.at[3 + d], 0, 2, d, 0)
 
     def tell_second():
         tell_wait(tell_recv, 0, tell_hop.at[pl.ds(4, 3)])
-        for d in (1, 3, 2):
+        for d in (2, 1, 3):
             tell_copy(tell_hop.at[pl.ds(3, 4), d], tell_mid.at[d - 1], 1, 1, d, 0)
 
     def tell_third():
         tell_wait(tell_recv, 1, tell_mid)
         for core in range(2):
-            for d in (1, 3, 2, 0):
+            for d in (2, 1, 3, 0):
                 if core or d:
                     tell_copy(tell_hop.at[pl.ds(3, 4), 0, d, core], told.at[core, d, 0], 3 - core, 0, d, core)
                     tell_copy(tell_mid.at[:, :, d, core], told.at[core, d, pl.ds(1, 3)], 3 - core, 0, d, core)

time: 83 us -> 83 us (level)
  no operation moved by 1% of the time
where the time goes in v7:
time: 83 us; the launch traced here: 82.9 us
  Pallas kernels  82 us (99%)
  local copies, waits for them, and re-layouts  0.88 us (1%)
    pallas_call x1, Pallas kernels, layer(): pl.pallas_call(kernel, out_shape=jax.ShapeDtypeStruct(hidden.shape, hidde...  82 us

profile of v7, /device:TPU:1, one launch (start us, length us, event | category | flops | bytes accessed | tf_op | source)
XLA Modules:
  0.0 82.9 jit_solution(6594759256494970186)
XLA Ops:
  0.0 82.0 %shard_map.46 = bf16[512,768]{1,0:T(8,128)(2,1)S(1)} custom-call(bf16[512,768]{1,0:T(8,128)(2,1)} %x_hbm.1, f32[512,128]{1,0:T(8,128)} %l_hbm.1, bf16[1,768,3072]{2,1,0:T(8,128)(2,1)} %win_hbm.1, bf16[1,3072,768]{2,1,0:T(8,128)(2,1)} %wout_hbm.1), custom_call_target="tpu_custom_call" | custom-call | tf_op jit(solution)/shard_map/pallas_call | solution.py:423
  82.0 0.9 %copy.6 = bf16[512,768]{1,0:T(8,128)(2,1)} copy(bf16[512,768]{1,0:T(8,128)(2,1)S(1)} %shard_map.46) | data formatting | bytes 1572864

commit v8 on v7

--- a/solution.py
+++ b/solution.py
@@ -343,6 +343,7 @@
     gather(1)
     inward.first(1)
     more()
+    gates()
     inward.first(3)
     tell_second()
     inward.second(0)
@@ -360,7 +361,7 @@
     during = {
         1: [lambda: inward.third(2)],
         4: [lambda: inward.third(3)],
-        7: [lambda: back.second(0)],
+        6: [lambda: back.second(0)],
         9: [lambda: back.second(1)],
     }
 
@@ -373,8 +374,11 @@
                 acc[...] = jnp.zeros_like(acc)
 
         at = pl.multiple_of(f * ftile, ftile)
-        h = gelu(dot(fin_i[c].reshape(rows, d_model), win[:, pl.ds(at, ftile)])).astype(BF16)
-        acc[...] += dot(h, wout[pl.ds(at, ftile), :])
+        chunk = fin_i[c].reshape(rows, d_model)
+        cut = rows // 2
+        up = [dot(chunk[r : r + cut], win[:, pl.ds(at, ftile)]) for r in (0, cut)]
+        for r, pre in zip((0, cut), up):
+            acc[r : r + cut] += dot(gelu(pre).astype(BF16), wout[pl.ds(at, ftile), :])
 
         for k in range(NCHUNK):
             @pl.when(i == k * FSTEPS + FSTEPS - 1)
@@ -390,13 +394,12 @@
 
     lax.fori_loop(0, NCHUNK * FSTEPS, step, 0)
 
+    back.second(2)
     back.third(0)
-    back.second(2)
-    gates()
     back.second(3)
+    back.third(2)
     back.third(1)
     combine(0)
-    back.third(2)
     back.third(3)
     combine(1)
     combine(2)

time: 83 us -> 84.8 us (1.022)
  Pallas kernels: 82 us -> 83.8 us
    pallas_call x1, Pallas kernels: 82 us -> 83.8 us  [layer(): pl.pallas_call(kernel, out_shape=jax.ShapeDtypeStruct(hidden.shape, hidde...]
where the time goes in v8:
time: 84.8 us; the launch traced here: 84.7 us
  Pallas kernels  83.8 us (99%)
  local copies, waits for them, and re-layouts  0.88 us (1%)
    pallas_call x1, Pallas kernels, layer(): pl.pallas_call(kernel, out_shape=jax.ShapeDtypeStruct(hidden.shape, hidde...  83.8 us

profile of v8, /device:TPU:1, one launch (start us, length us, event | category | flops | bytes accessed | tf_op | source)
XLA Modules:
  0.0 84.7 jit_solution(8847108924964411360)
XLA Ops:
  0.0 83.8 %shard_map.46 = bf16[512,768]{1,0:T(8,128)(2,1)S(1)} custom-call(bf16[512,768]{1,0:T(8,128)(2,1)} %x_hbm.1, f32[512,128]{1,0:T(8,128)} %l_hbm.1, bf16[1,768,3072]{2,1,0:T(8,128)(2,1)} %win_hbm.1, bf16[1,3072,768]{2,1,0:T(8,128)(2,1)} %wout_hbm.1), custom_call_target="tpu_custom_call" | custom-call | tf_op jit(solution)/shard_map/pallas_call | solution.py:426
  83.8 0.9 %copy.6 = bf16[512,768]{1,0:T(8,128)(2,1)} copy(bf16[512,768]{1,0:T(8,128)(2,1)S(1)} %shard_map.46) | data formatting | bytes 1572864

commit v9 on v7

--- a/solution.py
+++ b/solution.py
@@ -373,8 +373,11 @@
                 acc[...] = jnp.zeros_like(acc)
 
         at = pl.multiple_of(f * ftile, ftile)
-        h = gelu(dot(fin_i[c].reshape(rows, d_model), win[:, pl.ds(at, ftile)])).astype(BF16)
-        acc[...] += dot(h, wout[pl.ds(at, ftile), :])
+        chunk = fin_i[c].reshape(rows, d_model)
+        cut = rows // 2
+        up = [dot(chunk[r : r + cut], win[:, pl.ds(at, ftile)]) for r in (0, cut)]
+        for r, pre in zip((0, cut), up):
+            acc[r : r + cut] += dot(gelu(pre).astype(BF16), wout[pl.ds(at, ftile), :])
 
         for k in range(NCHUNK):
             @pl.when(i == k * FSTEPS + FSTEPS - 1)

time: 83 us -> 82.6 us (level)
  no operation moved by 1% of the time
where the time goes in v9:
time: 82.6 us; the launch traced here: 82.5 us
  Pallas kernels  81.6 us (99%)
  local copies, waits for them, and re-layouts  0.88 us (1%)
    pallas_call x1, Pallas kernels, layer(): pl.pallas_call(kernel, out_shape=jax.ShapeDtypeStruct(hidden.shape, hidde...  81.6 us

profile of v9, /device:TPU:1, one launch (start us, length us, event | category | flops | bytes accessed | tf_op | source)
XLA Modules:
  0.0 82.5 jit_solution(6004522261023883061)
XLA Ops:
  0.0 81.6 %shard_map.46 = bf16[512,768]{1,0:T(8,128)(2,1)S(1)} custom-call(bf16[512,768]{1,0:T(8,128)(2,1)} %x_hbm.1, f32[512,128]{1,0:T(8,128)} %l_hbm.1, bf16[1,768,3072]{2,1,0:T(8,128)(2,1)} %win_hbm.1, bf16[1,3072,768]{2,1,0:T(8,128)(2,1)} %wout_hbm.1), custom_call_target="tpu_custom_call" | custom-call | tf_op jit(solution)/shard_map/pallas_call | solution.py:426
  81.6 0.9 %copy.6 = bf16[512,768]{1,0:T(8,128)(2,1)} copy(bf16[512,768]{1,0:T(8,128)(2,1)S(1)} %shard_map.46) | data formatting | bytes 1572864
